TPU v7x, 128 devices: a whole 4x4x4 slice. The times are simulated.
128 devices in a mesh: items: 32 (over y, z, core), users: 4 (over x).
Axes of the slice: x: 4, y: 4, z: 4, core: 2. Of those that a mesh axis runs over, the one named last changes fastest.
Arguments:
- user_emb: bfloat16 [4096, 256], P('users', 'items'), as said below
- item_emb: bfloat16 [1048576, 256], P('items'), as said below
- target: int32 [4096], P('users'), may hold values from 0 to 1048575
- history: int32 [4096, 32], P('users'), may hold values from 0 to 1048575, as said below
Outputs:
- log_rank: float32 [4096], P('users')
- metrics: float32 [2], replicated
Inputs may be any that keep to these rules, and one draw needn't show every extreme that they name: history[u, k] lies in [k * 32768, (k + 1) * 32768); a user's history entries are thus distinct. `item_emb`: rows of norm about one. `user_emb`: entries of order one.
All inputs are finite; a program needn't handle non-finite values.
Results may differ from a plain program's by a relative error of at most 0.0003.
Values may be sent and summed in bfloat16 or wider, within the bound.
A program may use at most 64 MiB of HBM per device.

v0:
```python
import functools

import jax
import jax.numpy as jnp
from jax import lax
from jax.experimental import pallas as pl
from jax.experimental.pallas import tpu as pltpu
from jax.sharding import PartitionSpec as P

MESH = pl.DeviceIdType.MESH
CHUNK = 4096
GROUPS = 64
LOG_GROUPS = 6
WIDTH = 512
DOT = 512
PARTS = 2
PIECES = 8


def exchange(axis, n, me, src, dst, send, recv):
    copies = []
    for off in range(1, n):
        peer = lax.rem(me + off, n)
        copies.append(
            pltpu.make_async_remote_copy(
                src_ref=src,
                dst_ref=dst,
                send_sem=send.at[off - 1],
                recv_sem=recv.at[off - 1],
                device_id={axis: peer},
                device_id_type=MESH,
            )
        )
    for c in copies:
        c.start()
    return copies


def pick(tgt_ref, item_ref, own_ref, sem):
    item_dev = item_ref.shape[0]
    batch = 16

    def body(i, carry):
        for j in range(batch):
            user = i * batch + j
            local = lax.rem(tgt_ref[user], item_dev)
            row = pl.multiple_of((local >> 3) << 3, 8)
            pltpu.make_async_copy(
                item_ref.at[pl.ds(row, 8), :], own_ref.at[pl.ds(pl.multiple_of(user * 8, 8), 8), :], sem
            ).start()
        return carry

    u_dev = tgt_ref.shape[0]
    lax.fori_loop(0, u_dev // batch, body, 0)
    pltpu.make_async_copy(item_ref.at[pl.ds(0, u_dev * 8), :], own_ref, sem).wait()


def kernel(
    n, m, u_ref, own_ref, item_ref, tgt_ref, hist_ref, log_ref, met_ref,
    gath, w, items, own, tpart, tslots, apart, aslots, mpart, mslots, acc,
    sem_item, sem_own, sem_u, us, ur, ts, tr, as_, ar, ms, mr,
):
    me = lax.axis_index("items")
    grp = lax.axis_index("users")
    dsh, u_dev = u_ref.shape
    item_dev = item_ref.shape[0]
    per_shard = hist_ref.shape[0] // n
    span = item_dev // per_shard
    half = u_dev // PARTS
    piece = item_dev // PIECES

    fetches = []
    for i in range(PIECES):
        part = pl.ds(i * piece, piece)
        fetches.append(pltpu.make_async_copy(item_ref.at[part, :], items.at[part, :], sem_item.at[i]))
    mine = pl.ds(pl.multiple_of(me * dsh, dsh), dsh)
    keep = pltpu.make_async_copy(u_ref, gath.at[mine, :], sem_u)
    keep.start()
    tiles = pltpu.make_async_copy(own_ref, own, sem_own)
    tiles.start()
    for f in fetches:
        f.start()

    barrier = pltpu.get_barrier_semaphore()
    for off in range(1, n):
        pl.semaphore_signal(barrier, inc=1, device_id={"items": lax.rem(me + off, n)}, device_id_type=MESH)
    for off in range(1, m):
        pl.semaphore_signal(barrier, inc=1, device_id={"users": lax.rem(grp + off, m)}, device_id_type=MESH)
    pl.semaphore_wait(barrier, n - 1 + m - 1)

    ucopies = []
    for p in range(PARTS):
        cols = slice(p * half, (p + 1) * half)
        ucopies.append(exchange("items", n, me, u_ref.at[:, cols], gath.at[mine, cols], us.at[p], ur.at[p]))
    acc[...] = jnp.zeros_like(acc)
    keep.wait()
    tiles.wait()
    lane = lax.broadcasted_iota(jnp.int32, (8, 128), 1)
    sub = lax.broadcasted_iota(jnp.int32, (8, 128), 0)
    tcopies = []
    for p in range(PARTS):
        for c in ucopies[p]:
            c.wait()
        cols = slice(p * half, (p + 1) * half)
        w[:, cols] = gath[:, cols] * jnp.bfloat16(2)
        for b in range(half // 128):
            at = p * half + b * 128
            pc = jnp.dot(own[at * 8 : at * 8 + 1024, :], w[:, at : at + 128], preferred_element_type=jnp.float32)
            got = pc[:8]
            for r in range(1, 128):
                got = jnp.where(lane == r, pc[8 * r : 8 * r + 8], got)
            tgt = tgt_ref[:, at : at + 128]
            got = jnp.sum(jnp.where(sub == (tgt & 7), got, 0.0), axis=0, keepdims=True)
            local = tgt - me * item_dev
            tpart[p, :, b * 128 : (b + 1) * 128] = jnp.where((local >= 0) & (local < item_dev), got, 0.0)
        tslots[p, me] = tpart[p]
        tcopies.append(exchange("items", n, me, tpart.at[p], tslots.at[p, me], ts.at[p], tr.at[p]))

    rows = GROUPS * 8
    for f in fetches:
        f.wait()
    iota8 = lax.broadcasted_iota(jnp.int32, (8, WIDTH), 0)
    acopies = []
    for p in range(PARTS):
        for c in tcopies[p]:
            c.wait()
        tsum = tslots[p, 0]
        for i in range(1, n):
            tsum = tsum + tslots[p, i]
        tpart[p] = tsum

        def chunk(i, carry, p=p):
            k = lax.div(i * CHUNK, span)
            base = i * CHUNK - k * span
            row = me * per_shard + k
            for c in range(half // WIDTH):
                lo = p * half + c * WIDTH
                cols = slice(lo, lo + WIDTH)
                h = jnp.broadcast_to(hist_ref[pl.ds(row, 1), cols] - row * span, (8, WIDTH))
                t = jnp.broadcast_to(tpart[p, :, c * WIDTH : (c + 1) * WIDTH], (8, WIDTH))
                bits = [(h & (8 << b)) != 0 for b in range(LOG_GROUPS)]
                place = ((h >> (3 + LOG_GROUPS)) << 3) | (h & 7)
                total = acc[:, cols]
                for s in range(CHUNK // rows):
                    sums, picks = [], []
                    for q in range(rows // DOT):
                        at = pl.multiple_of(i * CHUNK + s * rows + q * DOT, DOT)
                        part = jnp.dot(items[pl.ds(at, DOT), :], w[:, cols], preferred_element_type=jnp.float32)
                        for g in range(DOT // 8):
                            tau = jnp.tanh(part[8 * g : 8 * g + 8] - t)
                            lvl, v = 0, tau
                            while sums and sums[-1][0] == lvl:
                                v = sums.pop()[1] + v
                                lvl += 1
                            if lvl == 2:
                                total = total + (v + 4.0)
                            else:
                                sums.append((lvl, v))
                            lvl, v = 0, tau
                            while picks and picks[-1][0] == lvl:
                                v = jnp.where(bits[lvl], v, picks.pop()[1])
                                lvl += 1
                            picks.append((lvl, v))
                    tile = lax.div(base, rows) + s
                    match = place == iota8 + tile * 8
                    total = total - jnp.where(match, picks[0][1] + 1.0, 0.0)
                acc[:, cols] = total
            return carry

        lax.fori_loop(0, item_dev // CHUNK, chunk, 0)
        cols = slice(p * half, (p + 1) * half)
        apart[p] = 0.5 * jnp.sum(acc[:, cols], axis=0, keepdims=True)
        aslots[p, me] = apart[p]
        acopies.append(exchange("items", n, me, apart.at[p], aslots.at[p, me], as_.at[p], ar.at[p]))

    seen = jnp.max(jnp.where(hist_ref[...] == tgt_ref[...], 1.0, 0.0), axis=0, keepdims=True)
    hs = jnp.zeros((1, 128), jnp.float32)
    gs = jnp.zeros((1, 128), jnp.float32)
    for p in range(PARTS):
        cols = slice(p * half, (p + 1) * half)
        for c in acopies[p]:
            c.wait()
        total = aslots[p, 0]
        for i in range(1, n):
            total = total + aslots[p, i]
        rank = 1.0 + (total - jnp.where(seen[:, cols] > 0.5, 0.0, 0.5))
        log_ref[:, cols] = jnp.log(rank)
        hit = jax.nn.sigmoid(10.5 - rank)
        gain = hit / jnp.log2(1.0 + rank)
        for b in range(half // 128):
            hs = hs + hit[:, b * 128 : (b + 1) * 128]
            gs = gs + gain[:, b * 128 : (b + 1) * 128]
    mpart[:, :128] = hs
    mpart[:, 128:] = gs
    mslots[grp] = mpart[...]
    copies = exchange("users", m, grp, mpart, mslots.at[grp], ms, mr)
    for c in copies:
        c.wait()
    tot = mslots[0]
    for i in range(1, m):
        tot = tot + mslots[i]
    scale = 1.0 / (u_dev * m)
    met_ref[0] = jnp.sum(tot[:, :128]) * scale
    met_ref[1] = jnp.sum(tot[:, 128:]) * scale


def solution(mesh):
    n, m = mesh.shape["items"], mesh.shape["users"]

    def body(user_emb, item_emb, target, history):
        u_dev, dsh = user_emb.shape
        item_dev, d = item_emb.shape
        half = u_dev // PARTS
        vmem = pl.BlockSpec(memory_space=pltpu.VMEM)
        hbm = pl.BlockSpec(memory_space=pltpu.HBM)
        dma = pltpu.SemaphoreType.DMA
        own = pl.pallas_call(
            pick,
            out_shape=jax.ShapeDtypeStruct((u_dev * 8, d), jnp.bfloat16),
            in_specs=[pl.BlockSpec(memory_space=pltpu.SMEM), pl.BlockSpec(memory_space=pltpu.HBM)],
            out_specs=vmem,
            scratch_shapes=[dma(())],
        )(target, item_emb)
        log_rank, metrics = pl.pallas_call(
            functools.partial(kernel, n, m),
            out_shape=(
                jax.ShapeDtypeStruct((1, u_dev), jnp.float32),
                jax.ShapeDtypeStruct((2,), jnp.float32),
            ),
            in_specs=[vmem, hbm, hbm, vmem, vmem],
            out_specs=(vmem, pl.BlockSpec(memory_space=pltpu.SMEM)),
            scratch_shapes=[
                pltpu.VMEM((d, u_dev), jnp.bfloat16),
                pltpu.VMEM((d, u_dev), jnp.bfloat16),
                pltpu.VMEM((item_dev, d), jnp.bfloat16),
                pltpu.VMEM((u_dev * 8, d), jnp.bfloat16),
                pltpu.VMEM((PARTS, 1, half), jnp.float32),
                pltpu.VMEM((PARTS, n, 1, half), jnp.float32),
                pltpu.VMEM((PARTS, 1, half), jnp.float32),
                pltpu.VMEM((PARTS, n, 1, half), jnp.float32),
                pltpu.VMEM((1, 256), jnp.float32),
                pltpu.VMEM((m, 1, 256), jnp.float32),
                pltpu.VMEM((8, u_dev), jnp.float32),
                dma((PIECES,)),
                dma(()),
                dma(()),
                dma((PARTS, n - 1)), dma((PARTS, n - 1)),
                dma((PARTS, n - 1)), dma((PARTS, n - 1)),
                dma((PARTS, n - 1)), dma((PARTS, n - 1)),
                dma((m - 1,)), dma((m - 1,)),
            ],
            compiler_params=pltpu.CompilerParams(
                collective_id=0, has_side_effects=True, vmem_limit_bytes=56 << 20
            ),
        )(user_emb.T, own, item_emb, target.reshape(1, u_dev), history.T)
        return log_rank.reshape(u_dev), metrics

    return jax.shard_map(
        body,
        mesh=mesh,
        in_specs=(P("users", "items"), P("items", None), P("users"), P("users", None)),
        out_specs=(P("users"), P()),
        check_vma=False,
    )
```

profile of v0, /device:TPU:1, one launch (start us, length us, event | category | flops | bytes accessed | tf_op | source)
XLA Modules:
  0.0 72.8 jit_solution(1711685820086278974)
XLA Ops:
  0.6 9.0 %shard_map.59.own_ref = bf16[8192,256]{1,0:T(8,128)(2,1)} custom-call(s32[1024]{0:T(1024)} %tgt_ref.1, bf16[32768,256]{1,0:T(8,128)(2,1)} %item_ref.3), custom_call_target="tpu_custom_call" | custom-call | tf_op jit(solution)/shard_map/pallas_call | solution.py:217
  9.7 60.7 %shard_map.60 = (f32[1,1024]{1,0:T(1,128)}, f32[2]{0:T(128)}) custom-call(bf16[8,1024]{1,0:T(8,128)(2,1)} %bitcast.5, bf16[8192,256]{1,0:T(8,128)(2,1)} %shard_map.59.own_ref, bf16[32768,256]{1,0:T(8,128)(2,1)} %item_ref.3, s32[1,1024]{1,0:T(1,128)} %bitcast.6, s32[32,1024]{1,0:T(8,128)} %bitcast.4), custom_call_target="tpu_custom_call" | custom-call | tf_op jit(solution)/shard_map/pallas_call | solution.py:224
  70.3 1.3 %copy.8 = f32[1024]{0:T(1024)} copy(f32[1024]{0:T(1024)} %bitcast.7) | data formatting | bytes 8192
  71.6 1.2 %copy.9 = f32[2]{0:T(128)} copy(f32[2]{0:T(128)} %get-tuple-element.9) | data formatting | bytes 16
where the time goes:
time: 73 us; the launch traced here: 72.8 us
  Pallas kernels  69.7 us (95%)
  local copies, waits for them, and re-layouts  2.45 us (3%)
    pallas_call x1, Pallas kernels, body(): pl.pallas_call(functools.partial(kernel, n, m), out_shape=(jax.ShapeDtype...  60.7 us
    pallas_call x1, Pallas kernels, body(): pl.pallas_call(pick, out_shape=jax.ShapeDtypeStruct((u_dev * 8, d), jnp.b...  9.02 us
    unnamed x2, local copies, waits for them, and re-layouts  2.45 us

commit v1 on v0

v1 whole, which is shorter than its diff:
```python
import functools

import jax
import jax.numpy as jnp
from jax import lax
from jax.experimental import pallas as pl
from jax.experimental.pallas import tpu as pltpu
from jax.sharding import PartitionSpec as P

MESH = pl.DeviceIdType.MESH
CHUNK = 4096
PARTS = 2
PIECES = 8
BATCH = 16
TILE = 16


def exchange(axis, n, me, src, dst, send, recv):
    copies = []
    for off in range(1, n):
        peer = lax.rem(me + off, n)
        copies.append(
            pltpu.make_async_remote_copy(
                src_ref=src,
                dst_ref=dst,
                send_sem=send.at[off - 1],
                recv_sem=recv.at[off - 1],
                device_id={axis: peer},
                device_id_type=MESH,
            )
        )
    for c in copies:
        c.start()
    return copies


def collect(ids, row, items, rows):
    tiles = items.shape[0]

    def body(i, carry):
        for j in range(BATCH):
            user = i * BATCH + j
            rows[user] = items[lax.rem(lax.div(ids[row, user], TILE), tiles)]
        return carry

    lax.fori_loop(0, ids.shape[1] // BATCH, body, 0)


def own_scores(rows, w, ids, at, width):
    lane = lax.broadcasted_iota(jnp.int32, (TILE, 128), 1)
    sub = lax.broadcasted_iota(jnp.int32, (TILE, 128), 0)
    d = rows.shape[2]
    out = []
    for b in range(width // 128):
        lo = at + b * 128
        pc = jnp.dot(
            rows[lo : lo + 128].reshape(128 * TILE, d), w[:, lo : lo + 128], preferred_element_type=jnp.float32
        )
        got = pc[:TILE]
        for r in range(1, 128):
            got = jnp.where(lane == r, pc[TILE * r : TILE * (r + 1)], got)
        here = sub == (ids[:, b * 128 : (b + 1) * 128] & (TILE - 1))
        out.append(jnp.sum(jnp.where(here, got, 0.0), axis=0, keepdims=True))
    return jnp.concatenate(out, axis=1)


def kernel(
    n, m, u_hbm, item_ref, tgt_hbm, hist_hbm, log_ref, met_ref,
    u_ref, tgt_ref, hist_ref, tid_ref, hid_ref, gath, w, items, rows, sa, sb, tpart, tslots, apart, aslots, mpart, mslots, hsc,
    sem_item, sem_in, us, ur, ts, tr, as_, ar, ms, mr,
):
    me = lax.axis_index("items")
    grp = lax.axis_index("users")
    dsh, u_dev = u_ref.shape
    d = item_ref.shape[2]
    item_dev = item_ref.shape[0] * TILE
    half = u_dev // PARTS
    piece = item_dev // TILE // PIECES

    ins = [
        pltpu.make_async_copy(u_hbm, u_ref, sem_in.at[0]),
        pltpu.make_async_copy(tgt_hbm, tgt_ref, sem_in.at[1]),
        pltpu.make_async_copy(hist_hbm, hist_ref, sem_in.at[2]),
        pltpu.make_async_copy(tgt_hbm, tid_ref, sem_in.at[3]),
        pltpu.make_async_copy(hist_hbm.at[pl.ds(pl.multiple_of(lax.div(me, 8) * 8, 8), 8), :], hid_ref, sem_in.at[4]),
    ]
    for c in ins:
        c.start()
    fetches = []
    for i in range(PIECES):
        part = pl.ds(i * piece, piece)
        fetches.append(pltpu.make_async_copy(item_ref.at[part], items.at[part], sem_item.at[i]))
    for f in fetches:
        f.start()

    barrier = pltpu.get_barrier_semaphore()
    for off in range(1, n):
        pl.semaphore_signal(barrier, inc=1, device_id={"items": lax.rem(me + off, n)}, device_id_type=MESH)
    for off in range(1, m):
        pl.semaphore_signal(barrier, inc=1, device_id={"users": lax.rem(grp + off, m)}, device_id_type=MESH)
    pl.semaphore_wait(barrier, n - 1 + m - 1)

    for c in ins:
        c.wait()
    ucopies = []
    for p in range(PARTS):
        cols = slice(p * half, (p + 1) * half)
        ucopies.append(exchange("items", n, me, u_ref.at[:, cols], gath.at[p, me], us.at[p], ur.at[p]))
        gath[p, me] = u_ref[:, cols]

    for f in fetches:
        f.wait()
    collect(tid_ref, 0, items, rows)

    tcopies = []
    for p in range(PARTS):
        for c in ucopies[p]:
            c.wait()
        cols = slice(p * half, (p + 1) * half)
        for i in range(n):
            w[i * dsh : (i + 1) * dsh, cols] = gath[p, i] * jnp.bfloat16(2)
        tgt = tgt_ref[:, cols]
        got = own_scores(rows, w, tgt, p * half, half)
        local = tgt - me * item_dev
        tpart[p] = jnp.where((local >= 0) & (local < item_dev), got, 0.0)
        tslots[p, me] = tpart[p]
        tcopies.append(exchange("items", n, me, tpart.at[p], tslots.at[p, me], ts.at[p], tr.at[p]))

    collect(hid_ref, lax.rem(me, 8), items, rows)
    for p in range(PARTS):
        cols = slice(p * half, (p + 1) * half)
        hsc[:, cols] = own_scores(rows, w, hist_ref[pl.ds(me, 1), cols], p * half, half)

    steps = item_dev // CHUNK

    def score(k, dst):
        at = lax.rem(k, steps) * (CHUNK // TILE)
        col = pl.multiple_of(lax.div(k, steps) * half, half)
        dst[...] = jnp.dot(
            items[pl.ds(at, CHUNK // TILE)].reshape(CHUNK, d), w[:, pl.ds(col, half)], preferred_element_type=jnp.float32
        )

    score(0, sa)
    acopies = []
    for p in range(PARTS):
        cols = slice(p * half, (p + 1) * half)
        for c in tcopies[p]:
            c.wait()
        tsum = tslots[p, 0]
        for i in range(1, n):
            tsum = tsum + tslots[p, i]
        t = jnp.broadcast_to(tsum, (8, half))

        def count(src, acc, t=t):
            sums = []
            for g in range(CHUNK // 8):
                v = jnp.tanh(src[8 * g : 8 * g + 8, :] - t) + 1.0
                lvl = 0
                while sums and sums[-1][0] == lvl and lvl < 3:
                    v = sums.pop()[1] + v
                    lvl += 1
                if lvl == 3:
                    acc = acc + v
                else:
                    sums.append((lvl, v))
            return acc

        def step(i, acc, p=p):
            k = p * steps + 2 * i
            score(k + 1, sb)
            acc = count(sa, acc)
            score(lax.rem(k + 2, PARTS * steps), sa)
            return count(sb, acc)

        acc = lax.fori_loop(0, steps // 2, step, jnp.zeros((8, half), jnp.float32))
        mine = jnp.tanh(hsc[:, cols] - tsum) + 1.0
        apart[p] = 0.5 * (jnp.sum(acc, axis=0, keepdims=True) - mine)
        aslots[p, me] = apart[p]
        acopies.append(exchange("items", n, me, apart.at[p], aslots.at[p, me], as_.at[p], ar.at[p]))

    seen = jnp.max(jnp.where(hist_ref[...] == tgt_ref[...], 1.0, 0.0), axis=0, keepdims=True)
    hs = jnp.zeros((1, 128), jnp.float32)
    gs = jnp.zeros((1, 128), jnp.float32)
    for p in range(PARTS):
        cols = slice(p * half, (p + 1) * half)
        for c in acopies[p]:
            c.wait()
        total = aslots[p, 0]
        for i in range(1, n):
            total = total + aslots[p, i]
        rank = 1.0 + (total - jnp.where(seen[:, cols] > 0.5, 0.0, 0.5))
        log_ref[:, cols] = jnp.log(rank)
        hit = jax.nn.sigmoid(10.5 - rank)
        gain = hit / jnp.log2(1.0 + rank)
        for b in range(half // 128):
            hs = hs + hit[:, b * 128 : (b + 1) * 128]
            gs = gs + gain[:, b * 128 : (b + 1) * 128]
    mpart[:, :128] = hs
    mpart[:, 128:] = gs
    mslots[grp] = mpart[...]
    copies = exchange("users", m, grp, mpart, mslots.at[grp], ms, mr)
    for c in copies:
        c.wait()
    tot = mslots[0]
    for i in range(1, m):
        tot = tot + mslots[i]
    scale = 1.0 / (u_dev * m)
    met_ref[0] = jnp.sum(tot[:, :128]) * scale
    met_ref[1] = jnp.sum(tot[:, 128:]) * scale


def solution(mesh):
    n, m = mesh.shape["items"], mesh.shape["users"]

    def body(user_emb, item_emb, target, history):
        u_dev, dsh = user_emb.shape
        item_dev, d = item_emb.shape
        half = u_dev // PARTS
        vmem = pl.BlockSpec(memory_space=pltpu.VMEM)
        smem = pl.BlockSpec(memory_space=pltpu.SMEM)
        hbm = pl.BlockSpec(memory_space=pltpu.HBM)
        dma = pltpu.SemaphoreType.DMA
        log_rank, metrics = pl.pallas_call(
            functools.partial(kernel, n, m),
            out_shape=(
                jax.ShapeDtypeStruct((1, u_dev), jnp.float32),
                jax.ShapeDtypeStruct((2,), jnp.float32),
            ),
            in_specs=[hbm, hbm, hbm, hbm],
            out_specs=(vmem, smem),
            scratch_shapes=[
                pltpu.VMEM((dsh, u_dev), jnp.bfloat16),
                pltpu.VMEM((1, u_dev), jnp.int32),
                pltpu.VMEM((history.shape[1], u_dev), jnp.int32),
                pltpu.SMEM((1, u_dev), jnp.int32),
                pltpu.SMEM((8, u_dev), jnp.int32),
                pltpu.VMEM((PARTS, n, dsh, half), jnp.bfloat16),
                pltpu.VMEM((d, u_dev), jnp.bfloat16),
                pltpu.VMEM((item_dev // TILE, TILE, d), jnp.bfloat16),
                pltpu.VMEM((u_dev, TILE, d), jnp.bfloat16),
                pltpu.VMEM((CHUNK, half), jnp.float32),
                pltpu.VMEM((CHUNK, half), jnp.float32),
                pltpu.VMEM((PARTS, 1, half), jnp.float32),
                pltpu.VMEM((PARTS, n, 1, half), jnp.float32),
                pltpu.VMEM((PARTS, 1, half), jnp.float32),
                pltpu.VMEM((PARTS, n, 1, half), jnp.float32),
                pltpu.VMEM((1, 256), jnp.float32),
                pltpu.VMEM((m, 1, 256), jnp.float32),
                pltpu.VMEM((1, u_dev), jnp.float32),
                dma((PIECES,)),
                dma((5,)),
                dma((PARTS, n - 1)), dma((PARTS, n - 1)),
                dma((PARTS, n - 1)), dma((PARTS, n - 1)),
                dma((PARTS, n - 1)), dma((PARTS, n - 1)),
                dma((m - 1,)), dma((m - 1,)),
            ],
            compiler_params=pltpu.CompilerParams(
                collective_id=0, has_side_effects=True, vmem_limit_bytes=60 << 20
            ),
        )(user_emb.T, item_emb.reshape(item_dev // TILE, TILE, d), target.reshape(1, u_dev), history.T)
        return log_rank.reshape(u_dev), metrics

    return jax.shard_map(
        body,
        mesh=mesh,
        in_specs=(P("users", "items"), P("items", None), P("users"), P("users", None)),
        out_specs=(P("users"), P()),
        check_vma=False,
    )
```

time: 73 us -> 66.4 us (0.910)
  Pallas kernels: 69.7 us -> 63.2 us
    pallas_call x1 -> x0, Pallas kernels: 9.02 us -> none  [body(): pl.pallas_call(pick, out_shape=jax.ShapeDtypeStruct((u_dev * 8, d), jnp.b...]
    pallas_call x1, Pallas kernels: 60.7 us -> 63.2 us  [body(): pl.pallas_call(functools.partial(kernel, n, m), out_shape=(jax.ShapeDtype...]
where the time goes in v1:
time: 66.4 us; the launch traced here: 66.2 us
  Pallas kernels  63.2 us (95%)
  local copies, waits for them, and re-layouts  2.4 us (4%)
    pallas_call x1, Pallas kernels, body(): pl.pallas_call(functools.partial(kernel, n, m), out_shape=(jax.ShapeDtype...  63.2 us
    unnamed x2, local copies, waits for them, and re-layouts  2.4 us

profile of v1, /device:TPU:1, one launch (start us, length us, event | category | flops | bytes accessed | tf_op | source)
XLA Modules:
  0.0 66.2 jit_solution(17222958848639744768)
XLA Ops:
  0.6 63.2 %shard_map.59 = (f32[1,1024]{1,0:T(1,128)}, f32[2]{0:T(128)}) custom-call(bf16[8,1024]{1,0:T(8,128)(2,1)} %bitcast.7, bf16[2048,16,256]{2,1,0:T(8,128)(2,1)} %bitcast.5, s32[1,1024]{1,0:T(1,128)} %bitcast.9, s32[32,1024]{1,0:T(8,128)} %bitcast.6), custom_call_target="tpu_custom_call" | custom-call | tf_op jit(solution)/shard_map/pallas_call | solution.py:223
  63.8 1.3 %copy.8 = f32[1024]{0:T(1024)} copy(f32[1024]{0:T(1024)} %bitcast.8) | data formatting | bytes 8192
  65.1 1.1 %copy.9 = f32[2]{0:T(128)} copy(f32[2]{0:T(128)} %get-tuple-element.9) | data formatting | bytes 16

commit v2 on v1

v2 whole, which is shorter than its diff:
```python
import functools

import jax
import jax.numpy as jnp
from jax import lax
from jax.experimental import pallas as pl
from jax.experimental.pallas import tpu as pltpu
from jax.sharding import PartitionSpec as P

MESH = pl.DeviceIdType.MESH
CHUNK = 8192
PART = 256
PIECES = 8
BATCH = 16
TILE = 16


def exchange(axis, peers, src, dst, send, recv):
    return [
        pltpu.make_async_remote_copy(
            src_ref=src,
            dst_ref=dst,
            send_sem=send.at[i],
            recv_sem=recv.at[i],
            device_id={axis: peer},
            device_id_type=MESH,
        )
        for i, peer in enumerate(peers)
    ]


def start(copies):
    for c in copies:
        c.start()


def wait(copies):
    for c in copies:
        c.wait()


def collect(ids, items, rows):
    tiles = items.shape[0]

    def body(i, carry):
        some = rows.at[pl.ds(i * BATCH, BATCH)]
        for j in range(BATCH):
            some[j] = items[(ids[0, i * BATCH + j] >> 4) & (tiles - 1)]
        return carry

    lax.fori_loop(0, ids.shape[1] // BATCH, body, 0)


def own_scores(rows, w, ids, out):
    d = rows.shape[2]
    lane = lax.broadcasted_iota(jnp.int32, (TILE, 128), 1)
    sub = lax.broadcasted_iota(jnp.int32, (TILE, 128), 0)

    def body(i, carry):
        cols = pl.ds(pl.multiple_of(i * 128, 128), 128)
        pc = jnp.dot(rows[cols].reshape(128 * TILE, d), w[:, cols], preferred_element_type=jnp.float32)
        got = pc[:TILE]
        for r in range(1, 128):
            got = jnp.where(lane == r, pc[TILE * r : TILE * (r + 1)], got)
        here = sub == (ids[:, cols] & (TILE - 1))
        out[:, cols] = jnp.sum(jnp.where(here, got, 0.0), axis=0, keepdims=True)
        return carry

    return body


def kernel(
    n, m, u_hbm, item_ref, tgt_hbm, hist_hbm, out_ref,
    tgt_ref, hist_ref, tid_ref, hid_ref, gath0, gath1, w, items, trows, hrows, sa, sb,
    tdot, tpart0, tpart1, tslots0, tslots1, tsum_ref, hsc, apart0, apart1, aslots0, aslots1, mpart, mslots,
    sem_item, sem_in, us, ur, fs, fr, ts, tr, as_, ar, ms, mr,
):
    me = lax.axis_index("items")
    grp = lax.axis_index("users")
    chip, core = lax.div(me, 2), lax.rem(me, 2)
    dsh, u_dev = u_hbm.shape
    d = item_ref.shape[2]
    item_dev = item_ref.shape[0] * TILE
    piece = item_dev // TILE // PIECES
    parts = u_dev // PART
    steps = item_dev // CHUNK
    peers = [lax.rem(me + off, n) for off in range(1, n)]
    twins = [lax.rem(me + 2 * off, n) for off in range(1, n // 2)]
    mates = [lax.rem(grp + off, m) for off in range(1, m)]
    other = [me + 1 - 2 * core]

    ins = [
        pltpu.make_async_copy(u_hbm.at[:, :PART], gath0.at[core, chip], sem_in.at[0]),
        pltpu.make_async_copy(u_hbm.at[:, PART:], gath1.at[core, chip], sem_in.at[1]),
        pltpu.make_async_copy(tgt_hbm, tgt_ref, sem_in.at[2]),
        pltpu.make_async_copy(hist_hbm, hist_ref, sem_in.at[3]),
        pltpu.make_async_copy(tgt_hbm, tid_ref, sem_in.at[4]),
        pltpu.make_async_copy(hist_hbm.at[pl.ds(me, 1), :], hid_ref, sem_in.at[5]),
    ]
    start(ins)
    fetches = []
    for i in range(PIECES):
        part = pl.ds(i * piece, piece)
        fetches.append(pltpu.make_async_copy(item_ref.at[part], items.at[part], sem_item.at[i]))
    start(fetches)

    barrier = pltpu.get_barrier_semaphore()
    for peer in peers:
        pl.semaphore_signal(barrier, inc=1, device_id={"items": peer}, device_id_type=MESH)
    for peer in mates:
        pl.semaphore_signal(barrier, inc=1, device_id={"users": peer}, device_id_type=MESH)
    wait(ins)
    pl.semaphore_wait(barrier, n - 1 + m - 1)

    groups = ((0, 0, PART, gath0, tpart0, tslots0), (1, PART, u_dev, gath1, tpart1, tslots1))
    ucopies, fcopies, tcopies = [], [], []
    for g, lo, hi, gath, tpart, tslots in groups:
        mine = gath.at[core, chip]
        near = peers if g == 0 else twins
        ucopies.append(exchange("items", near, mine, mine, us.at[g], ur.at[g]))
        fcopies.append(exchange("items", other if g else [], gath.at[core], gath.at[core], fs.at[g], fr.at[g]))
        tcopies.append(exchange("items", peers, tpart, tslots.at[me], ts.at[g], tr.at[g]))
        start(ucopies[g])

    wait(fetches)
    collect(tid_ref, items, trows)
    collect(hid_ref, items, hrows)

    pick_target = own_scores(trows, w, tgt_ref, tdot)
    for g, lo, hi, gath, tpart, tslots in groups:
        wait(ucopies[g])
        start(fcopies[g])
        wait(fcopies[g])
        for i in range(n // 2):
            both = jnp.concatenate([gath[0, i], gath[1, i]], axis=0)
            w[2 * i * dsh : 2 * (i + 1) * dsh, lo:hi] = both * jnp.bfloat16(2)
        lax.fori_loop(lo // 128, hi // 128, pick_target, 0)
        local = tgt_ref[:, lo:hi] - me * item_dev
        tpart[...] = jnp.where((local >= 0) & (local < item_dev), tdot[:, lo:hi], 0.0)
        tslots[me] = tpart[...]
        start(tcopies[g])

    pick_history = own_scores(hrows, w, hist_ref.at[pl.ds(me, 1), :], hsc)

    def score(k, dst):
        at = lax.rem(k, steps) * (CHUNK // TILE)
        col = pl.multiple_of(lax.div(k, steps) * PART, PART)
        dst[...] = jnp.dot(
            items[pl.ds(at, CHUNK // TILE)].reshape(CHUNK, d), w[:, pl.ds(col, PART)], preferred_element_type=jnp.float32
        )

    def count(src, acc, t):
        sums = []
        for g in range(CHUNK // 8):
            v = jnp.tanh(src[8 * g : 8 * g + 8, :] - t) + 1.0
            lvl = 0
            while sums and sums[-1][0] == lvl and lvl < 3:
                v = sums.pop()[1] + v
                lvl += 1
            if lvl == 3:
                acc = acc + v
            else:
                sums.append((lvl, v))
        return acc

    def total(p):
        cols = pl.ds(pl.multiple_of(p * PART, PART), PART)
        tsum = tsum_ref[:, cols]
        t = jnp.broadcast_to(tsum, (8, PART))

        def step(i, acc):
            k = p * steps + 2 * i
            pick_history(p * (PART // 128) + i, 0)
            score(k + 1, sb)
            acc = count(sa, acc, t)
            score(lax.rem(k + 2, parts * steps), sa)
            return count(sb, acc, t)

        acc = lax.fori_loop(0, steps // 2, step, jnp.zeros((8, PART), jnp.float32))
        mine = jnp.tanh(hsc[:, cols] - tsum) + 1.0
        return 0.5 * (jnp.sum(acc, axis=0, keepdims=True) - mine)

    def add(slots):
        out = slots[0]
        for i in range(1, n):
            out = out + slots[i]
        return out

    acopies = [
        exchange("items", peers, apart0, aslots0.at[me], as_.at[0], ar.at[0]),
        exchange("items", peers, apart1, aslots1.at[me], as_.at[1], ar.at[1]),
    ]

    def each(p, carry):
        @pl.when(p == 1)
        def _():
            wait(tcopies[1])
            tsum_ref[:, PART:] = add(tslots1)

        got = total(p)

        @pl.when(p < parts - 1)
        def _():
            apart0[:, pl.ds(pl.multiple_of(p * PART, PART), PART)] = got

        @pl.when(p == parts - 2)
        def _():
            aslots0[me] = apart0[...]
            start(acopies[0])

        @pl.when(p == parts - 1)
        def _():
            apart1[...] = got
            aslots1[me] = got
            start(acopies[1])

        return carry

    score(0, sa)
    wait(tcopies[0])
    tsum_ref[:, :PART] = add(tslots0)
    lax.fori_loop(0, parts, each, 0)

    seen = jnp.max(jnp.where(hist_ref[...] == tgt_ref[...], 1.0, 0.0), axis=0, keepdims=True)
    hs = jnp.zeros((1, 128), jnp.float32)
    gs = jnp.zeros((1, 128), jnp.float32)
    for g, lo, hi, aslots in ((0, 0, u_dev - PART, aslots0), (1, u_dev - PART, u_dev, aslots1)):
        wait(acopies[g])
        rank = 1.0 + (add(aslots) - jnp.where(seen[:, lo:hi] > 0.5, 0.0, 0.5))
        out_ref[:, lo:hi] = jnp.log(rank)
        hit = jax.nn.sigmoid(10.5 - rank)
        gain = hit / jnp.log2(1.0 + rank)
        for b in range((hi - lo) // 128):
            hs = hs + hit[:, b * 128 : (b + 1) * 128]
            gs = gs + gain[:, b * 128 : (b + 1) * 128]
    mpart[:, :128] = hs
    mpart[:, 128:] = gs
    mslots[grp] = mpart[...]
    copies = exchange("users", mates, mpart, mslots.at[grp], ms, mr)
    start(copies)
    wait(copies)
    tot = mslots[0]
    for i in range(1, m):
        tot = tot + mslots[i]
    scale = 1.0 / (u_dev * m)
    hs = jnp.sum(tot[:, :128], axis=1, keepdims=True) * scale
    gs = jnp.sum(tot[:, 128:], axis=1, keepdims=True) * scale
    out_ref[:, u_dev:] = jnp.where(lax.broadcasted_iota(jnp.int32, (1, 128), 1) == 0, hs, gs)


def split(both, log_ref, met_ref):
    u_dev = log_ref.shape[0]
    log_ref[...] = both[0, :u_dev]
    met_ref[...] = both[0, u_dev : u_dev + 2]


def solution(mesh):
    n, m = mesh.shape["items"], mesh.shape["users"]

    def body(user_emb, item_emb, target, history):
        u_dev, dsh = user_emb.shape
        item_dev, d = item_emb.shape
        vmem = pl.BlockSpec(memory_space=pltpu.VMEM)
        hbm = pl.BlockSpec(memory_space=pltpu.HBM)
        dma = pltpu.SemaphoreType.DMA
        rest = u_dev - PART
        f32, bf16, i32 = jnp.float32, jnp.bfloat16, jnp.int32
        both = pl.pallas_call(
            functools.partial(kernel, n, m),
            out_shape=jax.ShapeDtypeStruct((1, u_dev + 128), f32),
            in_specs=[hbm, hbm, hbm, hbm],
            out_specs=vmem,
            scratch_shapes=[
                pltpu.VMEM((1, u_dev), i32),
                pltpu.VMEM((history.shape[1], u_dev), i32),
                pltpu.SMEM((1, u_dev), i32),
                pltpu.SMEM((1, u_dev), i32),
                pltpu.VMEM((2, n // 2, dsh, PART), bf16),
                pltpu.VMEM((2, n // 2, dsh, rest), bf16),
                pltpu.VMEM((d, u_dev), bf16),
                pltpu.VMEM((item_dev // TILE, TILE, d), bf16),
                pltpu.VMEM((u_dev, TILE, d), bf16),
                pltpu.VMEM((u_dev, TILE, d), bf16),
                pltpu.VMEM((CHUNK, PART), f32),
                pltpu.VMEM((CHUNK, PART), f32),
                pltpu.VMEM((1, u_dev), f32),
                pltpu.VMEM((1, PART), f32),
                pltpu.VMEM((1, rest), f32),
                pltpu.VMEM((n, 1, PART), f32),
                pltpu.VMEM((n, 1, rest), f32),
                pltpu.VMEM((1, u_dev), f32),
                pltpu.VMEM((1, u_dev), f32),
                pltpu.VMEM((1, rest), f32),
                pltpu.VMEM((1, PART), f32),
                pltpu.VMEM((n, 1, rest), f32),
                pltpu.VMEM((n, 1, PART), f32),
                pltpu.VMEM((1, 256), f32),
                pltpu.VMEM((m, 1, 256), f32),
                dma((PIECES,)),
                dma((6,)),
                dma((2, n - 1)), dma((2, n - 1)),
                dma((2, 1)), dma((2, 1)),
                dma((2, n - 1)), dma((2, n - 1)),
                dma((2, n - 1)), dma((2, n - 1)),
                dma((m - 1,)), dma((m - 1,)),
            ],
            compiler_params=pltpu.CompilerParams(
                collective_id=0, has_side_effects=True, vmem_limit_bytes=60 << 20
            ),
        )(user_emb.T, item_emb.reshape(item_dev // TILE, TILE, d), target.reshape(1, u_dev), history.T)
        return pl.pallas_call(
            split,
            out_shape=(jax.ShapeDtypeStruct((u_dev,), f32), jax.ShapeDtypeStruct((2,), f32)),
            in_specs=[vmem],
            out_specs=(vmem, vmem),
        )(both)

    return jax.shard_map(
        body,
        mesh=mesh,
        in_specs=(P("users", "items"), P("items", None), P("users"), P("users", None)),
        out_specs=(P("users"), P()),
        check_vma=False,
    )
```

time: 66.4 us -> 60.9 us (0.917)
  Pallas kernels: 63.2 us -> 60.1 us
  local copies, waits for them, and re-layouts: 2.4 us -> 0 us
    pallas_call x1 -> x2, Pallas kernels: 63.2 us -> 60.1 us  [the longest x1 58.8 us: body(): pl.pallas_call(functools.partial(kernel, n, m), out_shape=jax.ShapeDtypeS...]
    unnamed x2 -> x0, local copies, waits for them, and re-layouts: 2.4 us -> none
where the time goes in v2:
time: 60.9 us; the launch traced here: 60.7 us
  Pallas kernels  60.1 us (99%)
  between operations  0.64 us (1%)
    pallas_call x1, Pallas kernels, body(): pl.pallas_call(functools.partial(kernel, n, m), out_shape=jax.ShapeDtypeS...  58.8 us
    pallas_call x1, Pallas kernels, body(): pl.pallas_call(split, out_shape=(jax.ShapeDtypeStruct((u_dev,), f32), jax...  1.28 us

profile of v2, /device:TPU:1, one launch (start us, length us, event | category | flops | bytes accessed | tf_op | source)
XLA Modules:
  0.0 60.7 jit_solution(9239175774414018650)
XLA Ops:
  0.6 58.8 %shard_map.59.both = f32[1,1152]{1,0:T(1,128)} custom-call(bf16[8,1024]{1,0:T(8,128)(2,1)} %bitcast.6, bf16[2048,16,256]{2,1,0:T(8,128)(2,1)} %bitcast.4, s32[1,1024]{1,0:T(1,128)} %bitcast.7, s32[32,1024]{1,0:T(8,128)} %bitcast.5), custom_call_target="tpu_custom_call" | custom-call | tf_op jit(solution)/shard_map/pallas_call | solution.py:268
  59.4 1.3 %shard_map.60 = (f32[1024]{0:T(1024)}, f32[2]{0:T(128)}) custom-call(f32[1,1152]{1,0:T(1,128)} %shard_map.59.both), custom_call_target="tpu_custom_call" | custom-call | tf_op jit(solution)/shard_map/pallas_call | solution.py:311

commit v3 on v2

--- a/solution.py
+++ b/solution.py
@@ -11,8 +11,8 @@
 CHUNK = 8192
 PART = 256
 PIECES = 8
-BATCH = 16
-TILE = 16
+BATCH = 32
+TILE = 8
 
 
 def exchange(axis, peers, src, dst, send, recv):
@@ -45,7 +45,7 @@
     def body(i, carry):
         some = rows.at[pl.ds(i * BATCH, BATCH)]
         for j in range(BATCH):
-            some[j] = items[(ids[0, i * BATCH + j] >> 4) & (tiles - 1)]
+            some[j] = items[(ids[0, i * BATCH + j] >> 3) & (tiles - 1)]
         return carry
 
     lax.fori_loop(0, ids.shape[1] // BATCH, body, 0)
@@ -124,12 +124,20 @@
 
     wait(fetches)
     collect(tid_ref, items, trows)
-    collect(hid_ref, items, hrows)
+
+    def score(k, dst):
+        at = lax.rem(k, steps) * (CHUNK // TILE)
+        col = pl.multiple_of(lax.div(k, steps) * PART, PART)
+        dst[...] = jnp.dot(
+            items[pl.ds(at, CHUNK // TILE)].reshape(CHUNK, d), w[:, pl.ds(col, PART)], preferred_element_type=jnp.float32
+        )
 
     pick_target = own_scores(trows, w, tgt_ref, tdot)
     for g, lo, hi, gath, tpart, tslots in groups:
         wait(ucopies[g])
         start(fcopies[g])
+        if g == 1:
+            score(0, sa)
         wait(fcopies[g])
         for i in range(n // 2):
             both = jnp.concatenate([gath[0, i], gath[1, i]], axis=0)
@@ -139,15 +147,10 @@
         tpart[...] = jnp.where((local >= 0) & (local < item_dev), tdot[:, lo:hi], 0.0)
         tslots[me] = tpart[...]
         start(tcopies[g])
+        if g == 0:
+            collect(hid_ref, items, hrows)
 
     pick_history = own_scores(hrows, w, hist_ref.at[pl.ds(me, 1), :], hsc)
-
-    def score(k, dst):
-        at = lax.rem(k, steps) * (CHUNK // TILE)
-        col = pl.multiple_of(lax.div(k, steps) * PART, PART)
-        dst[...] = jnp.dot(
-            items[pl.ds(at, CHUNK // TILE)].reshape(CHUNK, d), w[:, pl.ds(col, PART)], preferred_element_type=jnp.float32
-        )
 
     def count(src, acc, t):
         sums = []
@@ -216,7 +219,6 @@
 
         return carry
 
-    score(0, sa)
     wait(tcopies[0])
     tsum_ref[:, :PART] = add(tslots0)
     lax.fori_loop(0, parts, each, 0)

time: 60.9 us -> 58.9 us (0.967)
  Pallas kernels: 60.1 us -> 58.1 us
    pallas_call x1, Pallas kernels: 58.8 us -> 56.9 us  [body(): pl.pallas_call(functools.partial(kernel, n, m), out_shape=jax.ShapeDtypeS...]
where the time goes in v3:
time: 58.9 us; the launch traced here: 58.8 us
  Pallas kernels  58.1 us (99%)
  between operations  0.64 us (1%)
    pallas_call x1, Pallas kernels, body(): pl.pallas_call(functools.partial(kernel, n, m), out_shape=jax.ShapeDtypeS...  56.9 us
    pallas_call x1, Pallas kernels, body(): pl.pallas_call(split, out_shape=(jax.ShapeDtypeStruct((u_dev,), f32), jax...  1.28 us

profile of v3, /device:TPU:1, one launch (start us, length us, event | category | flops | bytes accessed | tf_op | source)
XLA Modules:
  0.0 58.8 jit_solution(10878315233787696341)
XLA Ops:
  0.6 56.9 %shard_map.59.both = f32[1,1152]{1,0:T(1,128)} custom-call(bf16[8,1024]{1,0:T(8,128)(2,1)} %bitcast.6, bf16[4096,8,256]{2,1,0:T(8,128)(2,1)} %bitcast.4, s32[1,1024]{1,0:T(1,128)} %bitcast.7, s32[32,1024]{1,0:T(8,128)} %bitcast.5), custom_call_target="tpu_custom_call" | custom-call | tf_op jit(solution)/shard_map/pallas_call | solution.py:270
  57.5 1.3 %shard_map.60 = (f32[1024]{0:T(1024)}, f32[2]{0:T(128)}) custom-call(f32[1,1152]{1,0:T(1,128)} %shard_map.59.both), custom_call_target="tpu_custom_call" | custom-call | tf_op jit(solution)/shard_map/pallas_call | solution.py:313

commit v4 on v3

--- a/solution.py
+++ b/solution.py
@@ -133,6 +133,12 @@
         )
 
     pick_target = own_scores(trows, w, tgt_ref, tdot)
+
+    def pick_part(i, carry):
+        for b in range(PART // 128):
+            carry = pick_target(i * (PART // 128) + b, carry)
+        return carry
+
     for g, lo, hi, gath, tpart, tslots in groups:
         wait(ucopies[g])
         start(fcopies[g])
@@ -142,7 +148,7 @@
         for i in range(n // 2):
             both = jnp.concatenate([gath[0, i], gath[1, i]], axis=0)
             w[2 * i * dsh : 2 * (i + 1) * dsh, lo:hi] = both * jnp.bfloat16(2)
-        lax.fori_loop(lo // 128, hi // 128, pick_target, 0)
+        lax.fori_loop(lo // PART, hi // PART, pick_part, 0)
         local = tgt_ref[:, lo:hi] - me * item_dev
         tpart[...] = jnp.where((local >= 0) & (local < item_dev), tdot[:, lo:hi], 0.0)
         tslots[me] = tpart[...]
@@ -173,9 +179,9 @@
 
         def step(i, acc):
             k = p * steps + 2 * i
-            pick_history(p * (PART // 128) + i, 0)
             score(k + 1, sb)
             acc = count(sa, acc, t)
+            pick_history(p * (PART // 128) + i, 0)
             score(lax.rem(k + 2, parts * steps), sa)
             return count(sb, acc, t)
 

time: 58.9 us -> 58.2 us (0.988)
  Pallas kernels: 58.1 us -> 57.5 us
    pallas_call x1, Pallas kernels: 56.9 us -> 56.2 us  [body(): pl.pallas_call(functools.partial(kernel, n, m), out_shape=jax.ShapeDtypeS...]
where the time goes in v4:
time: 58.2 us; the launch traced here: 58.1 us
  Pallas kernels  57.5 us (99%)
  between operations  0.64 us (1%)
    pallas_call x1, Pallas kernels, body(): pl.pallas_call(functools.partial(kernel, n, m), out_shape=jax.ShapeDtypeS...  56.2 us
    pallas_call x1, Pallas kernels, body(): pl.pallas_call(split, out_shape=(jax.ShapeDtypeStruct((u_dev,), f32), jax...  1.28 us

profile of v4, /device:TPU:1, one launch (start us, length us, event | category | flops | bytes accessed | tf_op | source)
XLA Modules:
  0.0 58.1 jit_solution(9802826491838467831)
XLA Ops:
  0.6 56.2 %shard_map.59.both = f32[1,1152]{1,0:T(1,128)} custom-call(bf16[8,1024]{1,0:T(8,128)(2,1)} %bitcast.6, bf16[4096,8,256]{2,1,0:T(8,128)(2,1)} %bitcast.4, s32[1,1024]{1,0:T(1,128)} %bitcast.7, s32[32,1024]{1,0:T(8,128)} %bitcast.5), custom_call_target="tpu_custom_call" | custom-call | tf_op jit(solution)/shard_map/pallas_call | solution.py:276
  56.8 1.3 %shard_map.60 = (f32[1024]{0:T(1024)}, f32[2]{0:T(128)}) custom-call(f32[1,1152]{1,0:T(1,128)} %shard_map.59.both), custom_call_target="tpu_custom_call" | custom-call | tf_op jit(solution)/shard_map/pallas_call | solution.py:319

commit v5 on v3

--- a/solution.py
+++ b/solution.py
@@ -124,6 +124,7 @@
 
     wait(fetches)
     collect(tid_ref, items, trows)
+    collect(hid_ref, items, hrows)
 
     def score(k, dst):
         at = lax.rem(k, steps) * (CHUNK // TILE)
@@ -133,6 +134,7 @@
         )
 
     pick_target = own_scores(trows, w, tgt_ref, tdot)
+
     for g, lo, hi, gath, tpart, tslots in groups:
         wait(ucopies[g])
         start(fcopies[g])
@@ -142,13 +144,18 @@
         for i in range(n // 2):
             both = jnp.concatenate([gath[0, i], gath[1, i]], axis=0)
             w[2 * i * dsh : 2 * (i + 1) * dsh, lo:hi] = both * jnp.bfloat16(2)
-        lax.fori_loop(lo // 128, hi // 128, pick_target, 0)
+        per = 2 if g == 0 else 3
+
+        def pick_some(i, carry, first=lo // 128, per=per):
+            for b in range(per):
+                carry = pick_target(first + i * per + b, carry)
+            return carry
+
+        lax.fori_loop(0, (hi - lo) // 128 // per, pick_some, 0)
         local = tgt_ref[:, lo:hi] - me * item_dev
         tpart[...] = jnp.where((local >= 0) & (local < item_dev), tdot[:, lo:hi], 0.0)
         tslots[me] = tpart[...]
         start(tcopies[g])
-        if g == 0:
-            collect(hid_ref, items, hrows)
 
     pick_history = own_scores(hrows, w, hist_ref.at[pl.ds(me, 1), :], hsc)
 
@@ -173,9 +180,9 @@
 
         def step(i, acc):
             k = p * steps + 2 * i
-            pick_history(p * (PART // 128) + i, 0)
             score(k + 1, sb)
             acc = count(sa, acc, t)
+            pick_history(p * (PART // 128) + i, 0)
             score(lax.rem(k + 2, parts * steps), sa)
             return count(sb, acc, t)
 

time: 58.9 us -> 58.3 us (0.990)
  Pallas kernels: 58.1 us -> 57.5 us
    pallas_call x1, Pallas kernels: 56.9 us -> 56.2 us  [body(): pl.pallas_call(functools.partial(kernel, n, m), out_shape=jax.ShapeDtypeS...]
where the time goes in v5:
time: 58.3 us; the launch traced here: 58.1 us
  Pallas kernels  57.5 us (99%)
  between operations  0.64 us (1%)
    pallas_call x1, Pallas kernels, body(): pl.pallas_call(functools.partial(kernel, n, m), out_shape=jax.ShapeDtypeS...  56.2 us
    pallas_call x1, Pallas kernels, body(): pl.pallas_call(split, out_shape=(jax.ShapeDtypeStruct((u_dev,), f32), jax...  1.28 us

profile of v5, /device:TPU:1, one launch (start us, length us, event | category | flops | bytes accessed | tf_op | source)
XLA Modules:
  0.0 58.1 jit_solution(9202796936144986466)
XLA Ops:
  0.6 56.2 %shard_map.59.both = f32[1,1152]{1,0:T(1,128)} custom-call(bf16[8,1024]{1,0:T(8,128)(2,1)} %bitcast.6, bf16[4096,8,256]{2,1,0:T(8,128)(2,1)} %bitcast.4, s32[1,1024]{1,0:T(1,128)} %bitcast.7, s32[32,1024]{1,0:T(8,128)} %bitcast.5), custom_call_target="tpu_custom_call" | custom-call | tf_op jit(solution)/shard_map/pallas_call | solution.py:277
  56.8 1.3 %shard_map.60 = (f32[1024]{0:T(1024)}, f32[2]{0:T(128)}) custom-call(f32[1,1152]{1,0:T(1,128)} %shard_map.59.both), custom_call_target="tpu_custom_call" | custom-call | tf_op jit(solution)/shard_map/pallas_call | solution.py:320
